TPU v7x, 32 devices: a whole 2x2x4 slice. The times are simulated.
32 devices in a mesh: member: 2 (over x), lat: 16 (over z, y, core).
Axes of the slice: x: 2, y: 2, z: 4, core: 2. Of those that a mesh axis runs over, the one named last changes fastest.
Arguments:
- height: float32 [128, 32, 1440], P(('member', 'lat')), parts along dimension 0, may hold values from -6 to 6
- zonal_courant: float32 [128, 32, 1440], P(('member', 'lat')), parts along dimension 0, may hold values from -1.5 to 1.5
- merid_courant: float32 [128, 32, 1440], P(('member', 'lat')), parts along dimension 0, may hold values from -1.5 to 1.5
- rates: float32 [64], P('member'), parts along dimension 0, may hold values from 0.05 to 0.5
- thresholds: float32 [64], P('member'), parts along dimension 0, may hold values from -3 to 3
- flags: int32 [64], replicated, may hold values from 0 to 1, as said below
- cutoffs: int32 [64], replicated, may hold values from 45 to 360
Outputs:
- filtered_height: float32 [128, 32, 1440], P(('member', 'lat')), parts along dimension 0
There are 2 independent parts, one for each index of `member`. A program takes and returns all parts, laid end to end along the dimension named above; an argument that names none is the same for every part. Nothing has to cross between parts.
Inputs may be any that keep to these rules, and one draw needn't show every extreme that they name: flags is 1 on a southern band of rows that starts at row 0 and on a northern band that ends at row 63, each band 64 // 8 to 16 rows long, and 0 on all other rows.
All inputs are finite; a program needn't handle non-finite values.
Results may differ from a plain program's by a relative error of at most 0.00007.
Values sent between devices are 32-bit elements; how exact they have to be, the bound alone decides.
No kernel may reach another device: no remote copies, remote signals or barrier semaphores. Data moves between devices by JAX's collectives and lax.ppermute only.
A program may use at most 64 MiB of HBM per device.

v0:
```python
import jax
import jax.numpy as jnp
from jax import lax
from jax.sharding import PartitionSpec as P


def padded_2(cells, sides, width):
    for axis, dim in sides:
        count = lax.axis_size(axis)
        ends = count - 1
        head = lax.slice_in_dim(cells, 0, width, axis=dim)
        tail = lax.slice_in_dim(cells, cells.shape[dim] - width, cells.shape[dim], axis=dim)
        cells = jnp.concatenate(
            [
                lax.ppermute(tail, axis, [(i, (i + 1) % count) for i in range(ends)]),
                cells,
                lax.ppermute(head, axis, [((i + 1) % count, i) for i in range(ends)]),
            ],
            axis=dim,
        )
    return cells


def transform_table(nlon, nkp):
    points = jnp.arange(nlon, dtype=jnp.int32)
    waves = jnp.arange(nkp, dtype=jnp.int32)
    phase = points[:, None] * waves[None, :] % nlon
    angle = 2.0 * jnp.pi / nlon * phase.astype(jnp.float32)
    return jnp.concatenate([jnp.cos(angle), jnp.sin(angle)], axis=1)


def wave_weights(nlon, nkp):
    waves = jnp.arange(nkp, dtype=jnp.int32)
    interior = jnp.where((waves > 0) & (waves < nlon // 2), 2.0, 1.0)
    return jnp.where(waves <= nlon // 2, interior, 0.0).astype(jnp.float32) / nlon


def damping(row_flags, row_cutoffs, nkp):
    waves = jnp.maximum(jnp.arange(nkp), 1).astype(jnp.float32)
    ratio = row_cutoffs.astype(jnp.float32)[:, None] / waves[None, :]
    factor = jnp.minimum(1.0, ratio * ratio)
    return jnp.where(row_flags[:, None] > 0, factor, 1.0)


def filter_units(flat, damp, table, weights):
    highest = lax.Precision.HIGHEST
    spectrum = jnp.dot(flat, table, precision=highest, preferred_element_type=jnp.float32)
    factor = (1.0 - damp) * weights[None, :]
    scaled = spectrum * jnp.concatenate([factor, factor], axis=1)
    dims = (((1,), (1,)), ((), ()))
    removed = lax.dot_general(
        scaled, table, dims, precision=highest, preferred_element_type=jnp.float32
    )
    return flat - removed


def filtered_or_kept(block, row_flags, row_cutoffs, table, weights):
    rows, levels, nlon = block.shape
    damp = damping(row_flags, row_cutoffs, weights.shape[0])
    unit_damp = jnp.broadcast_to(damp[:, None, :], (rows, levels, damp.shape[1])).reshape(
        rows * levels, damp.shape[1]
    )

    def apply_filter(data):
        return filter_units(data.reshape(rows * levels, nlon), unit_damp, table, weights).reshape(
            rows, levels, nlon
        )

    def keep_block(data):
        return data

    return lax.cond(jnp.any(row_flags > 0), apply_filter, keep_block, block)


def face_fluxes(rows_height, rows_speed, face_cos, count):
    face_value = (
        7.0 * (rows_height[1 : count + 1] + rows_height[2 : count + 2])
        - (rows_height[0:count] + rows_height[3 : count + 3])
    ) / 12.0
    speed = 0.5 * (rows_speed[0:count] + rows_speed[1 : count + 1]) * face_cos[:, None, None]
    return speed * face_value


def face_cosines(face_ids, nlat):
    return jnp.where(
        (face_ids > 0) & (face_ids < nlat),
        jnp.sin(jnp.pi * face_ids.astype(jnp.float32) / nlat),
        jnp.float32(0.0),
    )


def local(height, zonal_courant, merid_courant, rates, thresholds, flags, cutoffs):
    lat_rows, levels, nlon = height.shape
    devices = lax.axis_size("lat")
    position = lax.axis_index("lat")
    first_row = position * lat_rows
    nlat = lat_rows * devices
    local_rows = first_row + jnp.arange(lat_rows, dtype=jnp.int32)
    cos_rows = jnp.sin(jnp.pi * (local_rows.astype(jnp.float32) + 0.5) / nlat)
    faces = first_row + jnp.arange(lat_rows + 1, dtype=jnp.int32)
    cos_faces = face_cosines(faces, nlat)
    padded = padded_2(jnp.stack([height, merid_courant]), (("lat", 1),), 2)
    east = jnp.roll(height, -1, axis=2)
    west = jnp.roll(height, 1, axis=2)
    far_east = jnp.roll(height, -2, axis=2)
    face_height = (7.0 * (height + east) - (west + far_east)) / 12.0
    face_speed = 0.5 * (zonal_courant + jnp.roll(zonal_courant, -1, axis=2))
    zonal_flux = face_speed * face_height
    zonal_div = zonal_flux - jnp.roll(zonal_flux, 1, axis=2)
    source = -rates[None, :, None] * jax.nn.softplus(height - thresholds[None, :, None])
    partial_sums = jnp.sum(jnp.sum(source, axis=2) * cos_rows[:, None], axis=0)
    totals = lax.psum(partial_sums, "lat")
    all_rows = jnp.arange(nlat, dtype=jnp.int32)
    area = nlon * jnp.sum(jnp.sin(jnp.pi * (all_rows.astype(jnp.float32) + 0.5) / nlat))
    level_mean = totals / area
    padded_height = padded[0]
    padded_speed = padded[1]
    count = lat_rows + 1
    merid_flux = face_fluxes(padded_height, padded_speed[1:], cos_faces, count)
    merid_div = (merid_flux[1:] - merid_flux[:-1]) / cos_rows[:, None, None]
    updated = height - zonal_div - merid_div + source - level_mean[None, :, None]
    nkp = (nlon // 2 + 128) // 128 * 128
    table = transform_table(nlon, nkp)
    weights = wave_weights(nlon, nkp)
    row_flags = lax.dynamic_slice_in_dim(flags, first_row, lat_rows)
    row_cutoffs = lax.dynamic_slice_in_dim(cutoffs, first_row, lat_rows)
    result = filtered_or_kept(updated, row_flags, row_cutoffs, table, weights)
    return result


def solution(mesh):
    return jax.shard_map(
        local,
        mesh=mesh,
        in_specs=(
            P(("member", "lat"), None, None),
            P(("member", "lat"), None, None),
            P(("member", "lat"), None, None),
            P("member"),
            P("member"),
            P(),
            P(),
        ),
        out_specs=P(("member", "lat"), None, None),
        check_vma=False,
    )
```

profile of v0, /device:TPU:0, one launch (start us, length us, event | category | flops | bytes accessed | tf_op | source)
XLA Modules:
  0.0 101.5 jit_solution(3019089762479028692)
XLA Ops:
  0.0 0.0 copy-start
  0.0 0.0 copy-start.2
  0.0 2.8 %fusion.17 = (f32[2,2,32,1440]{3,2,1,0:T(8,128)}, f32[2,2,32,1440]{3,2,1,0:T(8,128)}) fusion(f32[1,4,32,1440]{3,2,1,0:T(8,128)} %bitcast.21, f32[1,4,32,1440]{3,2,1,0:T(8,128)} %bitcast.27), kind=kLoop, calls=%fused_computation.33 | loop fusion | flops 368640 | bytes 2949120 | tf_op jit(solution)/shard_map/stack | solution.py:102
  2.8 3.3 %collective-permute-start = (f32[2,2,32,1440]{3,2,1,0:T(8,128)}, f32[2,2,32,1440]{3,2,1,0:T(8,128)}, u32[]{:S(2)}, u32[]{:S(2)}) collective-permute-start(f32[2,2,32,1440]{3,2,1,0:T(8,128)} %get-tuple-element.115), channel_id=1, source_target_pairs={{0,1},{1,2},{2,3},{3,4},{4,5},{5,6},{6,7},{7,8},{8,9},{9,10},{10,1... | collective-permute-start | bytes 2211848 | tf_op jit(solution)/shard_map/ppermute | solution.py:15
  6.1 1.3 %collective-permute-start.1 = (f32[2,2,32,1440]{3,2,1,0:T(8,128)}, f32[2,2,32,1440]{3,2,1,0:T(8,128)}, u32[]{:S(2)}, u32[]{:S(2)}) collective-permute-start(f32[2,2,32,1440]{3,2,1,0:T(8,128)} %get-tuple-element.116), channel_id=1, source_target_pairs={{1,0},{2,1},{3,2},{4,3},{5,4},{6,5},{7,6},{8,7},{9,8},{10,9},{11,1... | collective-permute-start | bytes 2211848 | tf_op jit(solution)/shard_map/ppermute | solution.py:17
  7.3 2.8 %fusion.33 = (f32[4,32,1439]{2,1,0:T(8,128)}, f32[4,32,1439]{2,1,0:T(8,128)}) fusion(f32[4,32,1440]{2,1,0:T(8,128)} %param.9), kind=kLoop, calls=%fused_computation.63 | loop fusion | bytes 2947072 | tf_op jit(solution)/shard_map/jit(_roll_static)/slice | solution.py:104
  10.1 0.0 copy-done
  10.1 0.1 fusion.32
  10.2 0.3 slice.95
  10.5 0.0 copy-done.2
  10.5 1.2 %slice.89 = f32[4,32,1439]{2,1,0:T(8,128)} slice(f32[4,32,1440]{2,1,0:T(8,128)S(1)} %copy-done.2), slice={[0:4], [0:32], [1:1440]} | slice | bytes 1473536 | tf_op jit(solution)/shard_map/jit(_roll_static)/slice | solution.py:107
  11.8 0.7 sine_reduce_fusion
  12.4 0.0 copy-start.9
  12.4 0.0 slice-start
  12.4 0.0 copy-start.3
  12.4 0.0 copy-start.4
  12.4 0.0 copy-start.5
  12.4 0.0 copy-start.7
  12.5 19.6 %fusion.7 = (f32[1440,768]{1,0:T(8,128)}, f32[1440,768]{1,0:T(8,128)}) fusion(), kind=kLoop, calls=%fused_computation.15 | loop fusion | flops 9953280 | bytes 8847360 | tf_op jit(solution)/shard_map/sin | solution.py:29
  32.0 0.0 copy-start.8
  32.0 0.0 copy-start.10
  32.0 0.0 copy-done.9
  32.1 0.0 slice-done
  32.1 0.0 copy-done.3
  32.1 0.0 copy-done.4
  32.1 0.0 copy-done.5
  32.1 0.0 copy-done.7
  32.1 0.9 fusion.29
  33.0 0.1 multiply_reduce_fusion
  33.1 35.8 %psum.7 = f32[32]{0:T(128)S(1)} all-reduce(f32[32]{0:T(128)S(1)} %multiply_reduce_fusion), channel_id=1, replica_groups=mesh['member'=2,'lat'=16] {'lat'}, use_global_device_ids=true, to_apply=%region_3.4 | all-reduce | flops 32 | bytes 256 | tf_op jit(solution)/shard_map/psum | solution.py:112
  68.9 0.1 slice.109
  69.0 0.0 copy-done.8
  69.0 0.8 fusion.31
  69.8 0.0 copy-done.10
  69.8 0.1 dynamic-slice_convert_fusion
  71.2 0.0 copy-start.6
  71.2 8.2 %pad_maximum_fusion = f32[1440,1536]{1,0:T(8,128)} fusion(f32[1440,768]{1,0:T(8,128)} %get-tuple-element.123, f32[1440,768]{1,0:T(8,128)} %get-tuple-element.124), kind=kLoop, calls=%fused_computation.8 | loop fusion | flops 2211840 | bytes 17694720 | tf_op jit(solution)/shard_map/concatenate | solution.py:29
  79.4 0.0 collective-permute-done
  79.4 0.0 collective-permute-done.1
  79.4 0.0 copy-done.6
  79.4 1.9 %maximum_maximum_fusion = (f32[2,6,32,1440]{3,2,1,0:T(8,128)S(1)}, f32[2,6,32,1440]{3,2,1,0:T(8,128)S(1)}) fusion(f32[1,4,32,1440]{3,2,1,0:T(8,128)S(1)} %bitcast.28, f32[1,4,32,1440]{3,2,1,0:T(8,128)S(1)} %bitcast.22, f32[2,2,32,1440]{3,2,1,0:T(8,128)} %collective-permute-done, f32[2,2,32,1440]{3,2,1,0:T(8,128)} %collective-permute-done.1), kind=kLoop, calls=%fused_computation.18 | loop fusion | flops 2211840 | bytes 7372800 | tf_op jit(solution)/shard_map/concatenate | solution.py:13
  81.3 0.5 fusion.13
  81.8 0.7 fusion.22
  82.6 18.0 %conditional.1 = (f32[4,32,1440]{2,1,0:T(8,128)S(1)}) conditional(s32[]{:T(128)} %convert_element_type.42, f32[4,32,1440]{2,1,0:T(8,128)S(1)} %fusion.22, (f32[4,32,1440]{2,1,0:T(8,128)S(1)}, f32[1440,1536]{1,0:T(8,128)}, pred[4]{0:T(512)(128)(4,1)S(1)}, f32[4]{0:T(128)S(1)}, f32[1,768]{1,0:T(1,128)S(1)}, /*index=5*/s32[768]{0:T(1024)S(1)}) %tuple.45), branch_computations={%region_5.6_spmd, %region_6.7_spmd} | conditional | flops 6795468800 | bytes 25258016 | solution.py:72
  82.8 0.1 fusion.2
  82.9 7.6 %convolution_multiply_fusion = f32[128,1536]{1,0:T(8,128)S(1)} fusion(f32[128,1440]{1,0:T(8,128)S(1)} %bitcast.24, f32[1440,1536]{1,0:T(8,128)} %get-tuple-element.105, f32[128,768]{1,0:T(8,128)S(1)} %bitcast_multiply_fusion), kind=kOutput, calls=%fused_computation.1 | convolution fusion | flops 3397779456 | bytes 10764288 | tf_op jit(solution)/shard_map/cond/branch_1_fun/dot_general | solution.py:47
  90.6 0.3 copy.27
  90.8 9.5 %convolution_subtract_fusion = f32[128,1440]{0,1:T(8,128)S(1)} fusion(f32[128,1440]{0,1:T(8,128)S(1)} %copy.27, f32[128,1536]{1,0:T(8,128)S(1)} %convolution_multiply_fusion, f32[1440,1536]{1,0:T(8,128)} %get-tuple-element.105), kind=kOutput, calls=%fused_computation | convolution fusion | flops 3397570560 | bytes 11108352 | tf_op jit(solution)/shard_map/cond/branch_1_fun/dot_general | solution.py:51
  100.3 0.3 copy.28
  100.6 0.0 copy-start.1
  100.6 0.9 copy-done.1
  (10 shorter events, 0.2 us)
Async XLA Ops:
  0.0 10.1 %copy-start = (f32[4,32,1440]{2,1,0:T(8,128)S(1)}, f32[4,32,1440]{2,1,0:T(8,128)}, u32[]{:S(2)}) copy-start(f32[4,32,1440]{2,1,0:T(8,128)} %param.9) | copy-start | bytes 2211844
  0.0 10.5 %copy-start.2 = (f32[4,32,1440]{2,1,0:T(8,128)S(1)}, f32[4,32,1440]{2,1,0:T(8,128)}, u32[]{:S(2)}) copy-start(f32[4,32,1440]{2,1,0:T(8,128)} %param.10) | copy-start | bytes 2211844
  2.8 76.6 %collective-permute-start = (f32[2,2,32,1440]{3,2,1,0:T(8,128)}, f32[2,2,32,1440]{3,2,1,0:T(8,128)}, u32[]{:S(2)}, u32[]{:S(2)}) collective-permute-start(f32[2,2,32,1440]{3,2,1,0:T(8,128)} %get-tuple-element.115), channel_id=1, source_target_pairs={{0,1},{1,2},{2,3},{3,4},{4,5},{5,6},{6,7},{7,8},{8,9},{9,10},{10,1... | collective-permute-start | bytes 2211848 | tf_op jit(solution)/shard_map/ppermute | solution.py:15
  6.1 73.3 %collective-permute-start.1 = (f32[2,2,32,1440]{3,2,1,0:T(8,128)}, f32[2,2,32,1440]{3,2,1,0:T(8,128)}, u32[]{:S(2)}, u32[]{:S(2)}) collective-permute-start(f32[2,2,32,1440]{3,2,1,0:T(8,128)} %get-tuple-element.116), channel_id=1, source_target_pairs={{1,0},{2,1},{3,2},{4,3},{5,4},{6,5},{7,6},{8,7},{9,8},{10,9},{11,1... | collective-permute-start | bytes 2211848 | tf_op jit(solution)/shard_map/ppermute | solution.py:17
  12.4 19.6 %copy-start.9 = (f32[32]{0:T(128)S(1)}, f32[32]{0:T(128)}, u32[]{:S(2)}) copy-start(f32[32]{0:T(128)} %param.12) | copy-start | bytes 388
  12.4 19.6 %slice-start = ((f32[4,32,1440]{2,1,0:T(8,128)}), f32[4,32,1]{2,1,0:T(8,128)S(1)}, s32[]{:S(2)}) async-start(f32[4,32,1440]{2,1,0:T(8,128)} %param.10), calls=%async_computation | async-start | bytes 131072 | tf_op jit(solution)/shard_map/jit(_roll_static)/slice | solution.py:107
  12.4 19.7 %copy-start.3 = (f32[4,32,1439]{2,1,0:T(8,128)S(1)}, f32[4,32,1439]{2,1,0:T(8,128)}, u32[]{:S(2)}) copy-start(f32[4,32,1439]{2,1,0:T(8,128)} %slice.89) | copy-start | bytes 2210308
  12.4 19.7 %copy-start.4 = (f32[4,32,1439]{2,1,0:T(8,128)S(1)}, f32[4,32,1439]{2,1,0:T(8,128)}, u32[]{:S(2)}) copy-start(f32[4,32,1439]{2,1,0:T(8,128)} %get-tuple-element.121) | copy-start | bytes 2210308
  12.4 19.7 %copy-start.5 = (f32[4,32,1439]{2,1,0:T(8,128)S(1)}, f32[4,32,1439]{2,1,0:T(8,128)}, u32[]{:S(2)}) copy-start(f32[4,32,1439]{2,1,0:T(8,128)} %get-tuple-element.122) | copy-start | bytes 2210308
  12.4 19.7 %copy-start.7 = (f32[32]{0:T(128)S(1)}, f32[32]{0:T(128)}, u32[]{:S(2)}) copy-start(f32[32]{0:T(128)} %param.13) | copy-start | bytes 388
  32.0 37.0 %copy-start.8 = (s32[64]{0:T(128)S(1)}, s32[64]{0:T(128)}, u32[]{:S(2)}) copy-start(s32[64]{0:T(128)} %param.14) | copy-start | bytes 772
  32.0 37.8 %copy-start.10 = (s32[64]{0:T(128)S(1)}, s32[64]{0:T(128)}, u32[]{:S(2)}) copy-start(s32[64]{0:T(128)} %param.15) | copy-start | bytes 772
  71.2 8.2 %copy-start.6 = (f32[4,32,1440]{2,1,0:T(8,128)S(1)}, f32[4,32,1440]{2,1,0:T(8,128)}, u32[]{:S(2)}) copy-start(f32[4,32,1440]{2,1,0:T(8,128)} %param.11) | copy-start | bytes 2211844
  100.6 0.9 copy-start.1
where the time goes:
time: 102 us; the launch traced here: 101 us
  other arithmetic  36.4 us (36%)
  blocking collectives  35.8 us (35%)
  matrix products  17.1 us (17%)
  local copies, waits for them, and re-layouts  5.82 us (6%)
  starting transfers between devices  4.55 us (4%)
  between operations  1.52 us (1%)
    psum x1, blocking collectives, local(): totals = lax.psum(partial_sums, 'lat')  35.8 us
    sin x1, other arithmetic, transform_table(): return jnp.concatenate([jnp.cos(angle), jnp.sin(angle)], axis=1)  19.6 us
    dot_general x1, matrix products, filter_units(): lax.dot_general(scaled, table, dims, precision=highest, preferred_element...  9.48 us
    concatenate x1, other arithmetic, transform_table(): return jnp.concatenate([jnp.cos(angle), jnp.sin(angle)], axis=1)  8.16 us
    dot_general x1, matrix products, filter_units(): jnp.dot(flat, table, precision=highest, preferred_element_type=jnp.float32)  7.64 us
    ppermute x1, starting transfers between devices, padded_2(): lax.ppermute(tail, axis, [(i, (i + 1) % count) for i in range(ends)])  3.27 us
    slice x2, local copies, waits for them, and re-layouts, local(): west = jnp.roll(height, 1, axis=2)  2.85 us
    another operation x1, other arithmetic, local(): padded = padded_2(jnp.stack([height, merid_courant]), (('lat', 1),), 2)  2.78 us
  transfers between devices with their start and end apart: 2, of which 0 were waited for; matrix products, arithmetic and copies ran while one was open for 34% of the time, Pallas kernels for 0%

commit v1 on v0

--- a/solution.py
+++ b/solution.py
@@ -109,7 +109,9 @@
     zonal_div = zonal_flux - jnp.roll(zonal_flux, 1, axis=2)
     source = -rates[None, :, None] * jax.nn.softplus(height - thresholds[None, :, None])
     partial_sums = jnp.sum(jnp.sum(source, axis=2) * cos_rows[:, None], axis=0)
-    totals = lax.psum(partial_sums, "lat")
+    totals = partial_sums
+    for hop in (1, 2, 4, 8):
+        totals = totals + lax.ppermute(totals, "lat", [(dev, dev ^ hop) for dev in range(16)])
     all_rows = jnp.arange(nlat, dtype=jnp.int32)
     area = nlon * jnp.sum(jnp.sin(jnp.pi * (all_rows.astype(jnp.float32) + 0.5) / nlat))
     level_mean = totals / area

time: 102 us -> 81.8 us (0.80)
  blocking collectives: 35.8 us -> 0 us
  starting transfers between devices: 4.55 us -> 14.7 us
  waiting for transfers between devices: 0.01 us -> 2.8 us
  local copies, waits for them, and re-layouts: 5.82 us -> 7.93 us
    psum x1 -> x0, blocking collectives: 35.8 us -> none  [local(): totals = lax.psum(partial_sums, 'lat')]
    ppermute x0 -> x4, starting transfers between devices: none -> 10.5 us  [local(): lax.ppermute(totals, 'lat', [(dev, dev ^ hop) for dev in range(16)])]
    ppermute x0 -> x4, waiting for transfers between devices: none -> 2.79 us  [local(): lax.ppermute(totals, 'lat', [(dev, dev ^ hop) for dev in range(16)])]
    reduce_sum x2, other arithmetic: 1 us -> 2.59 us  [local(): partial_sums = jnp.sum(jnp.sum(source, axis=2) * cos_rows[:, None], axis=0)]
    slice x2 -> x3, local copies, waits for them, and re-layouts: 0.28 us -> 1.41 us  [local(): far_east = jnp.roll(height, -2, axis=2)]
  transfers between devices with their start and end apart: 2 -> 6, of which waited for: 0 -> 3; matrix products, arithmetic and copies ran while one was open for 34% -> 39% of each run, Pallas kernels for 0% -> 0%
where the time goes in v1:
time: 81.8 us; the launch traced here: 81.4 us
  other arithmetic  37.3 us (46%)
  matrix products  17.1 us (21%)
  starting transfers between devices  14.7 us (18%)
  local copies, waits for them, and re-layouts  7.93 us (10%)
  waiting for transfers between devices  2.8 us (3%)
  between operations  1.41 us (2%)
    sin x1, other arithmetic, transform_table(): return jnp.concatenate([jnp.cos(angle), jnp.sin(angle)], axis=1)  19.5 us
    ppermute x4, starting transfers between devices, local(): lax.ppermute(totals, 'lat', [(dev, dev ^ hop) for dev in range(16)])  10.5 us
    dot_general x1, matrix products, filter_units(): lax.dot_general(scaled, table, dims, precision=highest, preferred_element...  9.49 us
    concatenate x1, other arithmetic, transform_table(): return jnp.concatenate([jnp.cos(angle), jnp.sin(angle)], axis=1)  8.17 us
    dot_general x1, matrix products, filter_units(): jnp.dot(flat, table, precision=highest, preferred_element_type=jnp.float32)  7.6 us
    slice x2, local copies, waits for them, and re-layouts, local(): west = jnp.roll(height, 1, axis=2)  3.84 us
    ppermute x1, starting transfers between devices, padded_2(): lax.ppermute(tail, axis, [(i, (i + 1) % count) for i in range(ends)])  2.84 us
    ppermute x4, waiting for transfers between devices, local(): lax.ppermute(totals, 'lat', [(dev, dev ^ hop) for dev in range(16)])  2.79 us
  transfers between devices with their start and end apart: 6, of which 3 were waited for; matrix products, arithmetic and copies ran while one was open for 39% of the time, Pallas kernels for 0%

profile of v1, /device:TPU:0, one launch (start us, length us, event | category | flops | bytes accessed | tf_op | source)
XLA Modules:
  0.0 81.4 jit_solution(8887443526449307695)
XLA Ops:
  0.0 0.0 copy-start
  0.0 0.0 slice-start
  0.0 0.0 copy-start.2
  0.0 0.0 slice-start.1
  0.0 0.0 copy-start.6
  0.0 0.0 copy-start.4
  0.0 2.9 %fusion.33 = (f32[4,32,1439]{2,1,0:T(8,128)}, f32[4,32,1439]{2,1,0:T(8,128)}) fusion(f32[4,32,1440]{2,1,0:T(8,128)} %param.9), kind=kLoop, calls=%fused_computation.63 | loop fusion | bytes 2947072 | tf_op jit(solution)/shard_map/jit(_roll_static)/slice | solution.py:104
  2.9 1.0 %fusion.32 = (f32[4,32,1]{2,1,0:T(8,128)S(1)}, f32[4,32,1]{2,1,0:T(8,128)S(1)}) fusion(f32[4,32,1440]{2,1,0:T(8,128)} %param.9), kind=kLoop, calls=%fused_computation.62 | loop fusion | bytes 2048 | tf_op jit(solution)/shard_map/jit(_roll_static)/slice | solution.py:104
  3.9 1.4 %slice.95 = f32[4,32,1438]{2,1,0:T(8,128)S(1)} slice(f32[4,32,1440]{2,1,0:T(8,128)} %param.9), slice={[0:4], [0:32], [2:1440]} | slice | bytes 1472512 | tf_op jit(solution)/shard_map/jit(_roll_static)/slice | solution.py:105
  5.3 0.0 copy-done.2
  5.3 1.2 %slice.89 = f32[4,32,1439]{2,1,0:T(8,128)} slice(f32[4,32,1440]{2,1,0:T(8,128)S(1)} %copy-done.2), slice={[0:4], [0:32], [1:1440]} | slice | bytes 1473536 | tf_op jit(solution)/shard_map/jit(_roll_static)/slice | solution.py:107
  6.5 0.0 copy-done.6
  6.5 0.0 copy-done
  6.5 0.0 slice-done
  6.5 0.0 slice-done.1
  6.5 0.0 copy-done.4
  6.5 2.5 %fusion.29 = (f32[4,32]{1,0:T(4,128)S(1)}, f32[4,32,1440]{2,1,0:T(8,128)S(1)}) fusion(f32[4,32,1440]{2,1,0:T(8,128)S(1)} %copy-done, f32[32]{0:T(128)S(1)} %copy-done.4, f32[32]{0:T(128)S(1)} %neg.8, f32[4,32,2]{2,1,0:T(8,128)S(1)} %slice-done, f32[4,32,1438]{2,1,0:T(8,128)S(1)} %slice.95, f32[4,32,1439]{2,1,0:T(8,128)} %get-tuple-element.121, ...), kind=kLoop, calls=%fused_computation.51 | loop fusion | flops 3870592 | bytes 5161728 | tf_op jit(solution)/shard_map/reduce_sum | solution.py:111
  9.1 0.1 multiply_reduce_fusion
  9.1 0.5 collective-permute-start.2
  9.6 2.1 %fusion.17 = (f32[2,2,32,1440]{3,2,1,0:T(8,128)}, f32[2,2,32,1440]{3,2,1,0:T(8,128)S(1)}) fusion(f32[1,4,32,1440]{3,2,1,0:T(8,128)S(1)} %bitcast.21, f32[1,4,32,1440]{3,2,1,0:T(8,128)} %bitcast.27), kind=kLoop, calls=%fused_computation.33 | loop fusion | flops 368640 | bytes 2949120 | tf_op jit(solution)/shard_map/stack | solution.py:102
  11.8 2.8 %collective-permute-start = (f32[2,2,32,1440]{3,2,1,0:T(8,128)}, f32[2,2,32,1440]{3,2,1,0:T(8,128)}, u32[]{:S(2)}, u32[]{:S(2)}) collective-permute-start(f32[2,2,32,1440]{3,2,1,0:T(8,128)} %get-tuple-element.115), channel_id=1, source_target_pairs={{0,1},{1,2},{2,3},{3,4},{4,5},{5,6},{6,7},{7,8},{8,9},{9,10},{10,1... | collective-permute-start | bytes 2211848 | tf_op jit(solution)/shard_map/ppermute | solution.py:15
  14.6 1.3 %collective-permute-start.1 = (f32[2,2,32,1440]{3,2,1,0:T(8,128)S(1)}, f32[2,2,32,1440]{3,2,1,0:T(8,128)}, u32[]{:S(2)}, u32[]{:S(2)}) collective-permute-start(f32[2,2,32,1440]{3,2,1,0:T(8,128)S(1)} %get-tuple-element.116), channel_id=1, source_target_pairs={{1,0},{2,1},{3,2},{4,3},{5,4},{6,5},{7,6},{8,7},{9,8},{10,9},{11,1... | collective-permute-start | bytes 2211848 | tf_op jit(solution)/shard_map/ppermute | solution.py:17
  15.9 0.0 copy-start.5
  15.9 0.0 copy-start.7
  16.0 19.5 %fusion.7 = (f32[1440,768]{1,0:T(8,128)}, f32[1440,768]{1,0:T(8,128)}) fusion(), kind=kLoop, calls=%fused_computation.15 | loop fusion | flops 9953280 | bytes 8847360 | tf_op jit(solution)/shard_map/sin | solution.py:29
  35.5 0.0 copy-done.5
  35.5 0.8 fusion.31
  36.3 0.0 copy-done.7
  36.3 0.1 dynamic-slice_convert_fusion
  36.4 0.0 copy-start.3
  36.4 8.2 %pad_maximum_fusion = f32[1440,1536]{1,0:T(8,128)} fusion(f32[1440,768]{1,0:T(8,128)} %get-tuple-element.123, f32[1440,768]{1,0:T(8,128)} %get-tuple-element.124), kind=kLoop, calls=%fused_computation.8 | loop fusion | flops 2211840 | bytes 17694720 | tf_op jit(solution)/shard_map/concatenate | solution.py:29
  44.5 0.1 slice.109
  44.6 0.0 collective-permute-done.2
  44.6 4.0 %collective-permute-start.3 = (f32[32]{0:T(128)S(1)}, f32[32]{0:T(128)S(1)}, u32[]{:S(2)}, u32[]{:S(2)}) collective-permute-start(f32[32]{0:T(128)S(1)} %add.110), channel_id=1, source_target_pairs={{0,2},{1,3},{2,0},{3,1},{4,6},{5,7},{6,4},{7,5},{8,10},{9,11},{10,... | collective-permute-start | bytes 392 | tf_op jit(solution)/shard_map/ppermute | solution.py:114
  49.3 0.9 %collective-permute-done.3 = f32[32]{0:T(128)S(1)} collective-permute-done((f32[32]{0:T(128)S(1)}, f32[32]{0:T(128)S(1)}, u32[]{:S(2)}, u32[]{:S(2)}) %collective-permute-start.3) | collective-permute-done | bytes 160 | tf_op jit(solution)/shard_map/ppermute | solution.py:114
  50.2 3.0 %collective-permute-start.4 = (f32[32]{0:T(128)S(1)}, f32[32]{0:T(128)S(1)}, u32[]{:S(2)}, u32[]{:S(2)}) collective-permute-start(f32[32]{0:T(128)S(1)} %add.111), channel_id=1, source_target_pairs={{0,4},{1,5},{2,6},{3,7},{4,0},{5,1},{6,2},{7,3},{8,12},{9,13},{10,... | collective-permute-start | bytes 392 | tf_op jit(solution)/shard_map/ppermute | solution.py:114
  53.2 0.6 sine_reduce_fusion
  53.8 0.9 %collective-permute-done.4 = f32[32]{0:T(128)S(1)} collective-permute-done((f32[32]{0:T(128)S(1)}, f32[32]{0:T(128)S(1)}, u32[]{:S(2)}, u32[]{:S(2)}) %collective-permute-start.4) | collective-permute-done | bytes 160 | tf_op jit(solution)/shard_map/ppermute | solution.py:114
  54.7 3.0 %collective-permute-start.5 = (f32[32]{0:T(128)S(1)}, f32[32]{0:T(128)S(1)}, u32[]{:S(2)}, u32[]{:S(2)}) collective-permute-start(f32[32]{0:T(128)S(1)} %add.112), channel_id=1, source_target_pairs={{0,8},{1,9},{2,10},{3,11},{4,12},{5,13},{6,14},{7,15},{8,0},{9,1},... | collective-permute-start | bytes 392 | tf_op jit(solution)/shard_map/ppermute | solution.py:114
  58.3 1.0 %collective-permute-done.5 = f32[32]{0:T(128)S(1)} collective-permute-done((f32[32]{0:T(128)S(1)}, f32[32]{0:T(128)S(1)}, u32[]{:S(2)}, u32[]{:S(2)}) %collective-permute-start.5) | collective-permute-done | bytes 160 | tf_op jit(solution)/shard_map/ppermute | solution.py:114
  59.3 0.0 collective-permute-done
  59.3 0.0 collective-permute-done.1
  59.3 0.0 copy-done.3
  59.3 1.9 %maximum_maximum_fusion = (f32[2,6,32,1440]{3,2,1,0:T(8,128)S(1)}, f32[2,6,32,1440]{3,2,1,0:T(8,128)S(1)}) fusion(f32[1,4,32,1440]{3,2,1,0:T(8,128)S(1)} %bitcast.28, f32[1,4,32,1440]{3,2,1,0:T(8,128)S(1)} %bitcast.22, f32[2,2,32,1440]{3,2,1,0:T(8,128)} %collective-permute-done, f32[2,2,32,1440]{3,2,1,0:T(8,128)} %collective-permute-done.1), kind=kLoop, calls=%fused_computation.18 | loop fusion | flops 2211840 | bytes 7372800 | tf_op jit(solution)/shard_map/concatenate | solution.py:13
  61.3 0.5 fusion.13
  61.8 0.7 fusion.22
  62.5 18.0 %conditional.1 = (f32[4,32,1440]{2,1,0:T(8,128)S(1)}) conditional(s32[]{:T(128)} %convert_element_type.42, f32[4,32,1440]{2,1,0:T(8,128)S(1)} %fusion.22, (f32[4,32,1440]{2,1,0:T(8,128)S(1)}, f32[1440,1536]{1,0:T(8,128)}, pred[4]{0:T(512)(128)(4,1)S(1)}, f32[4]{0:T(128)S(1)}, f32[1,768]{1,0:T(1,128)S(1)}, /*index=5*/s32[768]{0:T(1024)S(1)}) %tuple.45), branch_computations={%region_4.5_spmd, %region_5.6_spmd} | conditional | flops 6795468800 | bytes 25258016 | solution.py:72
  62.8 0.1 fusion.2
  62.9 7.6 %convolution_multiply_fusion = f32[128,1536]{1,0:T(8,128)S(1)} fusion(f32[128,1440]{1,0:T(8,128)S(1)} %bitcast.24, f32[1440,1536]{1,0:T(8,128)} %get-tuple-element.105, f32[128,768]{1,0:T(8,128)S(1)} %bitcast_multiply_fusion), kind=kOutput, calls=%fused_computation.1 | convolution fusion | flops 3397779456 | bytes 10764288 | tf_op jit(solution)/shard_map/cond/branch_1_fun/dot_general | solution.py:47
  70.5 0.3 copy.27
  70.8 9.5 %convolution_subtract_fusion = f32[128,1440]{0,1:T(8,128)S(1)} fusion(f32[128,1440]{0,1:T(8,128)S(1)} %copy.27, f32[128,1536]{1,0:T(8,128)S(1)} %convolution_multiply_fusion, f32[1440,1536]{1,0:T(8,128)} %get-tuple-element.105), kind=kOutput, calls=%fused_computation | convolution fusion | flops 3397570560 | bytes 11108352 | tf_op jit(solution)/shard_map/cond/branch_1_fun/dot_general | solution.py:51
  80.3 0.3 copy.28
  80.5 0.0 copy-start.1
  80.5 0.9 %copy-done.1 = f32[4,32,1440]{2,1,0:T(8,128)} copy-done((f32[4,32,1440]{2,1,0:T(8,128)}, f32[4,32,1440]{2,1,0:T(8,128)S(1)}, u32[]{:S(2)}) %copy-start.1) | copy-done | bytes 737304
  (12 shorter events, 0.2 us)
Async XLA Ops:
  0.0 6.5 %copy-start = (f32[4,32,1440]{2,1,0:T(8,128)S(1)}, f32[4,32,1440]{2,1,0:T(8,128)}, u32[]{:S(2)}) copy-start(f32[4,32,1440]{2,1,0:T(8,128)} %param.9) | copy-start | bytes 2211844
  0.0 6.5 %slice-start = ((f32[4,32,1440]{2,1,0:T(8,128)}), f32[4,32,2]{2,1,0:T(8,128)S(1)}, s32[]{:S(2)}) async-start(f32[4,32,1440]{2,1,0:T(8,128)} %param.9), calls=%async_computation | async-start | bytes 131072 | tf_op jit(solution)/shard_map/jit(_roll_static)/slice | solution.py:105
  0.0 5.3 %copy-start.2 = (f32[4,32,1440]{2,1,0:T(8,128)S(1)}, f32[4,32,1440]{2,1,0:T(8,128)}, u32[]{:S(2)}) copy-start(f32[4,32,1440]{2,1,0:T(8,128)} %param.10) | copy-start | bytes 2211844
  0.0 6.5 %slice-start.1 = ((f32[4,32,1440]{2,1,0:T(8,128)}), f32[4,32,1]{2,1,0:T(8,128)S(1)}, s32[]{:S(2)}) async-start(f32[4,32,1440]{2,1,0:T(8,128)} %param.10), calls=%async_computation.1 | async-start | bytes 131072 | tf_op jit(solution)/shard_map/jit(_roll_static)/slice | solution.py:107
  0.0 6.4 %copy-start.6 = (f32[32]{0:T(128)S(1)}, f32[32]{0:T(128)}, u32[]{:S(2)}) copy-start(f32[32]{0:T(128)} %param.12) | copy-start | bytes 388
  0.0 6.5 %copy-start.4 = (f32[32]{0:T(128)S(1)}, f32[32]{0:T(128)}, u32[]{:S(2)}) copy-start(f32[32]{0:T(128)} %param.13) | copy-start | bytes 388
  9.1 35.5 %collective-permute-start.2 = (f32[32]{0:T(128)S(1)}, f32[32]{0:T(128)S(1)}, u32[]{:S(2)}, u32[]{:S(2)}) collective-permute-start(f32[32]{0:T(128)S(1)} %multiply_reduce_fusion), channel_id=1, source_target_pairs={{0,1},{1,0},{2,3},{3,2},{4,5},{5,4},{6,7},{7,6},{8,9},{9,8},{10,11... | collective-permute-start | bytes 392 | tf_op jit(solution)/shard_map/ppermute | solution.py:114
  11.8 47.6 %collective-permute-start = (f32[2,2,32,1440]{3,2,1,0:T(8,128)}, f32[2,2,32,1440]{3,2,1,0:T(8,128)}, u32[]{:S(2)}, u32[]{:S(2)}) collective-permute-start(f32[2,2,32,1440]{3,2,1,0:T(8,128)} %get-tuple-element.115), channel_id=1, source_target_pairs={{0,1},{1,2},{2,3},{3,4},{4,5},{5,6},{6,7},{7,8},{8,9},{9,10},{10,1... | collective-permute-start | bytes 2211848 | tf_op jit(solution)/shard_map/ppermute | solution.py:15
  14.6 44.7 %collective-permute-start.1 = (f32[2,2,32,1440]{3,2,1,0:T(8,128)S(1)}, f32[2,2,32,1440]{3,2,1,0:T(8,128)}, u32[]{:S(2)}, u32[]{:S(2)}) collective-permute-start(f32[2,2,32,1440]{3,2,1,0:T(8,128)S(1)} %get-tuple-element.116), channel_id=1, source_target_pairs={{1,0},{2,1},{3,2},{4,3},{5,4},{6,5},{7,6},{8,7},{9,8},{10,9},{11,1... | collective-permute-start | bytes 2211848 | tf_op jit(solution)/shard_map/ppermute | solution.py:17
  15.9 19.6 %copy-start.5 = (s32[64]{0:T(128)S(1)}, s32[64]{0:T(128)}, u32[]{:S(2)}) copy-start(s32[64]{0:T(128)} %param.14) | copy-start | bytes 772
  15.9 20.3 %copy-start.7 = (s32[64]{0:T(128)S(1)}, s32[64]{0:T(128)}, u32[]{:S(2)}) copy-start(s32[64]{0:T(128)} %param.15) | copy-start | bytes 772
  36.4 23.0 %copy-start.3 = (f32[4,32,1440]{2,1,0:T(8,128)S(1)}, f32[4,32,1440]{2,1,0:T(8,128)}, u32[]{:S(2)}) copy-start(f32[4,32,1440]{2,1,0:T(8,128)} %param.11) | copy-start | bytes 2211844
  44.6 5.6 %collective-permute-start.3 = (f32[32]{0:T(128)S(1)}, f32[32]{0:T(128)S(1)}, u32[]{:S(2)}, u32[]{:S(2)}) collective-permute-start(f32[32]{0:T(128)S(1)} %add.110), channel_id=1, source_target_pairs={{0,2},{1,3},{2,0},{3,1},{4,6},{5,7},{6,4},{7,5},{8,10},{9,11},{10,... | collective-permute-start | bytes 392 | tf_op jit(solution)/shard_map/ppermute | solution.py:114
  50.2 4.5 %collective-permute-start.4 = (f32[32]{0:T(128)S(1)}, f32[32]{0:T(128)S(1)}, u32[]{:S(2)}, u32[]{:S(2)}) collective-permute-start(f32[32]{0:T(128)S(1)} %add.111), channel_id=1, source_target_pairs={{0,4},{1,5},{2,6},{3,7},{4,0},{5,1},{6,2},{7,3},{8,12},{9,13},{10,... | collective-permute-start | bytes 392 | tf_op jit(solution)/shard_map/ppermute | solution.py:114
  54.7 4.6 %collective-permute-start.5 = (f32[32]{0:T(128)S(1)}, f32[32]{0:T(128)S(1)}, u32[]{:S(2)}, u32[]{:S(2)}) collective-permute-start(f32[32]{0:T(128)S(1)} %add.112), channel_id=1, source_target_pairs={{0,8},{1,9},{2,10},{3,11},{4,12},{5,13},{6,14},{7,15},{8,0},{9,1},... | collective-permute-start | bytes 392 | tf_op jit(solution)/shard_map/ppermute | solution.py:114
  80.5 0.9 %copy-start.1 = (f32[4,32,1440]{2,1,0:T(8,128)}, f32[4,32,1440]{2,1,0:T(8,128)S(1)}, u32[]{:S(2)}) copy-start(f32[4,32,1440]{2,1,0:T(8,128)S(1)} %get-tuple-element.127) | copy-start | bytes 2211844
